TPU v7x, 256 devices: a whole 4x4x8 slice. The times are simulated.
256 devices in a mesh: row: 32 (over y, z), col: 8 (over x, core).
Axes of the slice: x: 4, y: 4, z: 8, core: 2. Of those that a mesh axis runs over, the one named last changes fastest.
Arguments:
- activations: float32 [512, 12288], P('col', 'row'), may hold values from -1.5 to 1.5
- weights: float32 [12288, 24576], P('row', 'col'), may hold values from -0.21875 to 0.21875
- upstream: float32 [512, 24576], P('row', 'col'), may hold values from -6 to 6
Outputs:
- input_grad: float32 [512, 12288], P('col', 'row')
- weight_grad: float32 [12288, 24576], P('row', 'col')
All inputs are finite; a program needn't handle non-finite values.
Results may differ from a plain program's by a relative error of at most 0.00009.
Values sent between devices are 32-bit elements; how exact they have to be, the bound alone decides.
No kernel may reach another device: no remote copies, remote signals or barrier semaphores. Data moves between devices by JAX's collectives and lax.ppermute only.
A program may use at most 64 MiB of HBM per device.

v0:
```python
import jax
import jax.numpy as jnp
from jax import lax
from jax.sharding import Mesh
from jax.sharding import PartitionSpec as P

COL = ("col_0", "col_1")
ROW = ("row_0", "row_1")
slope_scale = 0.7978845608028654
cubic_term = 0.044715


def in_order(blocks, dim):
    blocks = jnp.moveaxis(blocks, 0, dim)
    shape = blocks.shape
    return blocks.reshape(*shape[:dim], shape[dim] * shape[dim + 1], *shape[dim + 2 :])


def all_blocks(x, axes, turns):
    blocks = x[None]
    for k in turns:
        blocks = lax.all_gather(blocks, axes[k], axis=0, tiled=True)
    held = [lax.axis_size(axes[k]) for k in reversed(turns)]
    blocks = blocks.reshape(*held, *x.shape)
    turned = sorted(range(len(turns)), key=lambda place: turns[len(turns) - 1 - place])
    return blocks.transpose(*turned, *range(len(turns), blocks.ndim)).reshape(-1, *x.shape)


def gather_axes(x, axes, turns, dim):
    return in_order(all_blocks(x, axes, turns), dim)


def summed_rows(x, axes, dim):
    for axis in axes:
        x = lax.psum_scatter(x, axis, scatter_dimension=dim, tiled=True)
    return x


def in_blocks(x, dim, length):
    before, after = (x.shape[:dim], x.shape[dim + 1 :])
    return jnp.moveaxis(x.reshape(*before, length, -1, *after), dim, 0)


def summed_on_arrival(x, axis, dim):
    blocks = in_blocks(x, dim, lax.axis_size(axis))
    arrived = lax.all_to_all(blocks, axis, split_axis=0, concat_axis=0, tiled=True)
    return arrived.sum(axis=0)


def gelu_slope(preact):
    inner = slope_scale * (preact + cubic_term * preact * preact * preact)
    tangent = jnp.tanh(inner)
    return 0.5 * (1.0 + tangent) + 0.5 * preact * (1.0 - tangent * tangent) * slope_scale * (
        1.0 + 3.0 * cubic_term * preact * preact
    )


def body(activations, weights, upstream):
    gathered = gather_axes(activations, COL, (0, 1), 0)
    partial_pre = jnp.dot(
        gathered, weights, precision=lax.Precision.HIGHEST, preferred_element_type=jnp.float32
    )
    shares = summed_rows(partial_pre, ROW, 0)
    delta_pre = lax.all_gather(upstream * gelu_slope(shares), ROW, axis=0, tiled=True)
    weight_grad = lax.dot_general(
        gathered,
        delta_pre,
        (((0,), (0,)), ((), ())),
        precision=lax.Precision.HIGHEST,
        preferred_element_type=jnp.float32,
    )
    input_grad = summed_on_arrival(
        lax.dot_general(
            delta_pre,
            weights,
            (((1,), (1,)), ((), ())),
            precision=lax.Precision.HIGHEST,
            preferred_element_type=jnp.float32,
        ),
        COL,
        0,
    )
    return (input_grad, weight_grad)


def solution(mesh):
    torus = Mesh(mesh.devices.reshape(4, 8, 4, 2), ("row_0", "row_1", "col_0", "col_1"))
    in_specs = (P(COL, ROW), P(ROW, COL), P(ROW, COL))
    out_specs = (P(COL, ROW), P(ROW, COL))
    return jax.shard_map(body, mesh=torus, in_specs=in_specs, out_specs=out_specs, check_vma=False)
```

profile of v0, /device:TPU:1, one launch (start us, length us, event | category | flops | bytes accessed | tf_op | source)
XLA Modules:
  0.0 285.1 jit_solution(7580726740365344956)
XLA Ops:
  7.2 0.0 reduce-scatter.3.cloned.1.call-start
  7.2 11.9 %all-gather = f32[256,384]{1,0:T(8,128)S(1)} all-gather(f32[64,384]{1,0:T(8,128)} %param.3), channel_id=2, replica_groups=mesh['row_0'=4,'row_1'=8,'col_0'=4,'col_1'=2] {'col_0'}, dimensions={0}, use_global_device_ids=true | all-gather | bytes 491520 | tf_op jit(solution)/shard_map/all_gather | solution.py:22
  19.1 6.4 %all_gather.10 = f32[8,64,384]{2,1,0:T(8,128)S(1)} all-gather(f32[4,64,384]{2,1,0:T(8,128)S(1)} %bitcast.17), channel_id=1, replica_groups=mesh['row_0'=4,'row_1'=8,'col_0'=4,'col_1'=2] {'col_1'}, dimensions={0}, use_global_device_ids=true | all-gather | bytes 1179648 | tf_op jit(solution)/shard_map/all_gather | solution.py:22
  25.5 0.1 copy.9
  25.6 13.6 %fusion.6 = f32[512,3072]{1,0:T(8,128)} fusion(f32[512,384]{1,0:T(8,128)S(1)} %bitcast.14, f32[384,3072]{1,0:T(8,128)} %param.4), kind=kOutput, calls=%fused_computation.9 | convolution fusion | flops 7247757312 | bytes 11796480 | tf_op jit(solution)/shard_map/dot_general | solution.py:60
  39.2 0.0 copy-start
  39.2 0.0 reduce-scatter.3.cloned.1.call-update
  39.2 0.0 reduce-scatter.5.cloned.1.call-start
  39.3 67.3 %reduce-scatter.3.cloned.1.call-done = f32[128,3072]{1,0:T(8,128)} async-done(((f32[512,3072]{1,0:T(8,128)}), f32[128,3072]{1,0:T(8,128)}) %reduce-scatter.3.cloned.1.call-update) | async-done | bytes 1572880 | tf_op jit(solution)/shard_map/reduce_scatter | solution.py:35
  106.6 0.0 reduce-scatter.5.cloned.1.call-update
  106.6 0.0 all-gather.3.cloned.1.call-start
  106.6 39.0 %reduce-scatter.5.cloned.1.call-done = f32[16,3072]{1,0:T(8,128)} async-done(((f32[128,3072]{1,0:T(8,128)}), f32[16,3072]{1,0:T(8,128)}) %reduce-scatter.5.cloned.1.call-update) | async-done | bytes 196624 | tf_op jit(solution)/shard_map/reduce_scatter | solution.py:35
  145.7 0.0 copy-done
  145.7 1.7 fusion.5
  147.4 0.0 all-gather.3.cloned.1.call-update
  147.4 91.2 %all-gather.3.cloned.1.call-done = f32[512,3072]{1,0:T(8,128)} async-done(((f32[16,3072]{1,0:T(8,128)}), f32[512,3072]{1,0:T(8,128)}) %all-gather.3.cloned.1.call-update) | async-done | bytes 6291472 | tf_op jit(solution)/shard_map/all_gather | solution.py:64
  238.7 13.8 %fusion.7 = f32[512,384]{1,0:T(8,128)} fusion(f32[512,3072]{1,0:T(8,128)} %all-gather.3.cloned.1.call-done, f32[384,3072]{1,0:T(8,128)} %param.4), kind=kOutput, calls=%fused_computation.10 | convolution fusion | flops 7247757312 | bytes 11796480 | tf_op jit(solution)/shard_map/dot_general | solution.py:73
  252.4 5.9 %all-to-all-start = ((f32[8,64,384]{2,1,0:T(8,128)}), f32[8,64,384]{2,1,0:T(8,128)S(1)}, u32[]{:S(2)}, u32[]{:S(2)}) async-start(f32[8,64,384]{2,1,0:T(8,128)} %bitcast.4), calls=%async_computation.2 | async-start | bytes 1572864 | tf_op jit(solution)/shard_map/all_to_all | solution.py:46
  258.3 13.6 %convolution_bitcast_fusion = f32[384,3072]{0,1:T(8,128)} fusion(f32[512,3072]{1,0:T(8,128)} %all-gather.3.cloned.1.call-done, f32[512,384]{1,0:T(8,128)S(1)} %bitcast.15), kind=kOutput, calls=%fused_computation | convolution fusion | flops 7247757312 | bytes 11796480 | tf_op jit(solution)/shard_map/dot_general | solution.py:65
  271.9 6.0 %copy.10 = f32[384,3072]{1,0:T(8,128)} copy(f32[384,3072]{0,1:T(8,128)} %convolution_bitcast_fusion) | data formatting | bytes 9437184
  277.9 0.0 all-to-all-done
  277.9 0.7 reduce_sum.9
Async XLA Ops:
  7.2 99.4 %reduce-scatter.3.cloned.1.call-start = ((), (), s32[]{:S(2)}) async-start(), calls=%async_computation.3 | async-start | bytes 7864320 | tf_op jit(solution)/shard_map/reduce_scatter | solution.py:35
  39.2 106.5 %copy-start = (f32[16,3072]{1,0:T(8,128)S(1)}, f32[16,3072]{1,0:T(8,128)}, u32[]{:S(2)}) copy-start(f32[16,3072]{1,0:T(8,128)} %param.5) | copy-start | bytes 589828
  39.2 106.5 %reduce-scatter.5.cloned.1.call-start = ((), (), s32[]{:S(2)}) async-start(), calls=%async_computation.4 | async-start | bytes 1769472 | tf_op jit(solution)/shard_map/reduce_scatter | solution.py:35
  106.6 132.1 %all-gather.3.cloned.1.call-start = ((), (), s32[]{:S(2)}) async-start(), calls=%async_computation.5 | async-start | bytes 6488064 | tf_op jit(solution)/shard_map/all_gather | solution.py:64
  252.4 25.5 %all-to-all-start = ((f32[8,64,384]{2,1,0:T(8,128)}), f32[8,64,384]{2,1,0:T(8,128)S(1)}, u32[]{:S(2)}, u32[]{:S(2)}) async-start(f32[8,64,384]{2,1,0:T(8,128)} %bitcast.4), calls=%async_computation.2 | async-start | bytes 1572864 | tf_op jit(solution)/shard_map/all_to_all | solution.py:46
Sparse Core Ops, SparseCore 0:
  39.3 67.1 reduce-scatter.2
  109.1 36.5 reduce-scatter.4
  148.8 89.7 all-gather.2
where the time goes:
time: 285 us
  waiting for transfers between devices  198 us (69%)
  matrix products  41 us (14%)
  blocking collectives  18.3 us (6%)
  between operations  13.8 us (5%)
  local copies, waits for them, and re-layouts  6.1 us (2%)
  starting transfers between devices  5.97 us (2%)
    reduce_scatter x2, waiting for transfers between devices, summed_rows(): x = lax.psum_scatter(x, axis, scatter_dimension=dim, tiled=True)  106 us
    all_gather x1, waiting for transfers between devices, body(): lax.all_gather(upstream * gelu_slope(shares), ROW, axis=0, tiled=True)  91.2 us
    all_gather x2, blocking collectives, all_blocks(): blocks = lax.all_gather(blocks, axes[k], axis=0, tiled=True)  18.3 us
    dot_general x1, matrix products, body(): lax.dot_general(delta_pre, weights, (((1,), (1,)), ((), ())), precision=l...  13.8 us
    dot_general x1, matrix products, body(): jnp.dot(gathered, weights, precision=lax.Precision.HIGHEST, preferred_ele...  13.6 us
    dot_general x1, matrix products, body(): lax.dot_general(gathered, delta_pre, (((0,), (0,)), ((), ())), precision=...  13.6 us
    unnamed x3, local copies, waits for them, and re-layouts  6.05 us
    all_to_all x1, starting transfers between devices, summed_on_arrival(): lax.all_to_all(blocks, axis, split_axis=0, concat_axis=0, tiled=True)  5.85 us
  transfers between devices with their start and end apart: 4, of which 3 were waited for; matrix products, arithmetic and copies ran while one was open for 7% of the time, Pallas kernels for 0%

commit v1 on v0

--- a/solution.py
+++ b/solution.py
@@ -61,7 +61,9 @@
         gathered, weights, precision=lax.Precision.HIGHEST, preferred_element_type=jnp.float32
     )
     shares = summed_rows(partial_pre, ROW, 0)
-    delta_pre = lax.all_gather(upstream * gelu_slope(shares), ROW, axis=0, tiled=True)
+    part = upstream * gelu_slope(shares)
+    repeated = jnp.stack([part] * lax.axis_size(ROW))
+    delta_pre = jnp.concatenate(lax.all_to_all(repeated, ROW, 0, 0), axis=0)
     weight_grad = lax.dot_general(
         gathered,
         delta_pre,

time: 285 us -> 342 us (1.20)
  blocking collectives: 18.3 us -> 158 us
  waiting for transfers between devices: 198 us -> 106 us
  starting transfers between devices: 5.97 us -> 13.5 us
    all_to_all x0 -> x1, blocking collectives: none -> 140 us  [body(): delta_pre = jnp.concatenate(lax.all_to_all(repeated, ROW, 0, 0), axis=0)]
    all_gather x1 -> x0, waiting for transfers between devices: 91.2 us -> none  [body(): lax.all_gather(upstream * gelu_slope(shares), ROW, axis=0, tiled=True)]
    all_to_all x1, starting transfers between devices: 5.85 us -> 13.4 us  [summed_on_arrival(): lax.all_to_all(blocks, axis, split_axis=0, concat_axis=0, tiled=True)]
    unnamed x3 -> x9, local copies, waits for them, and re-layouts: 6.05 us -> 8.71 us
  transfers between devices with their start and end apart: 4 -> 3, of which waited for: 3 -> 2; matrix products, arithmetic and copies ran while one was open for 7% -> 6% of each run, Pallas kernels for 0% -> 0%
where the time goes in v1:
time: 342 us
  blocking collectives  158 us (46%)
  waiting for transfers between devices  106 us (31%)
  matrix products  38.2 us (11%)
  between operations  14.1 us (4%)
  starting transfers between devices  13.5 us (4%)
  local copies, waits for them, and re-layouts  9.51 us (3%)
    all_to_all x1, blocking collectives, body(): delta_pre = jnp.concatenate(lax.all_to_all(repeated, ROW, 0, 0), axis=0)  140 us
    reduce_scatter x2, waiting for transfers between devices, summed_rows(): x = lax.psum_scatter(x, axis, scatter_dimension=dim, tiled=True)  106 us
    all_gather x2, blocking collectives, all_blocks(): blocks = lax.all_gather(blocks, axes[k], axis=0, tiled=True)  18.3 us
    dot_general x1, matrix products, body(): jnp.dot(gathered, weights, precision=lax.Precision.HIGHEST, preferred_ele...  13.6 us
    dot_general x1, matrix products, body(): lax.dot_general(gathered, delta_pre, (((0,), (0,)), ((), ())), precision=...  13.6 us
    all_to_all x1, starting transfers between devices, summed_on_arrival(): lax.all_to_all(blocks, axis, split_axis=0, concat_axis=0, tiled=True)  13.4 us
    dot_general x1, matrix products, body(): lax.dot_general(delta_pre, weights, (((1,), (1,)), ((), ())), precision=l...  11 us
    unnamed x9, local copies, waits for them, and re-layouts  8.71 us
  transfers between devices with their start and end apart: 3, of which 2 were waited for; matrix products, arithmetic and copies ran while one was open for 6% of the time, Pallas kernels for 0%

profile of v1, /device:TPU:1, one launch (start us, length us, event | category | flops | bytes accessed | tf_op | source)
XLA Modules:
  0.0 341.9 jit_solution(10398972300342429925)
XLA Ops:
  7.2 0.0 reduce-scatter.3.cloned.1.call-start
  7.2 11.9 %all-gather = f32[256,384]{1,0:T(8,128)S(1)} all-gather(f32[64,384]{1,0:T(8,128)} %param.3), channel_id=2, replica_groups=mesh['row_0'=4,'row_1'=8,'col_0'=4,'col_1'=2] {'col_0'}, dimensions={0}, use_global_device_ids=true | all-gather | bytes 491520 | tf_op jit(solution)/shard_map/all_gather | solution.py:22
  19.1 6.4 %all_gather.7 = f32[8,64,384]{2,1,0:T(8,128)S(1)} all-gather(f32[4,64,384]{2,1,0:T(8,128)S(1)} %bitcast.24), channel_id=1, replica_groups=mesh['row_0'=4,'row_1'=8,'col_0'=4,'col_1'=2] {'col_1'}, dimensions={0}, use_global_device_ids=true | all-gather | bytes 1179648 | tf_op jit(solution)/shard_map/all_gather | solution.py:22
  25.5 0.1 copy.9
  25.6 13.6 %fusion.8 = f32[512,3072]{1,0:T(8,128)} fusion(f32[512,384]{1,0:T(8,128)S(1)} %bitcast.21, f32[384,3072]{1,0:T(8,128)} %param.4), kind=kOutput, calls=%fused_computation.11 | convolution fusion | flops 7247757312 | bytes 11796480 | tf_op jit(solution)/shard_map/dot_general | solution.py:60
  39.2 0.0 copy-start.1
  39.2 0.0 reduce-scatter.3.cloned.1.call-update
  39.2 0.0 reduce-scatter.5.cloned.1.call-start
  39.3 67.3 %reduce-scatter.3.cloned.1.call-done = f32[128,3072]{1,0:T(8,128)} async-done(((f32[512,3072]{1,0:T(8,128)}), f32[128,3072]{1,0:T(8,128)}) %reduce-scatter.3.cloned.1.call-update) | async-done | bytes 1572880 | tf_op jit(solution)/shard_map/reduce_scatter | solution.py:35
  106.6 0.0 reduce-scatter.5.cloned.1.call-update
  106.6 39.1 %reduce-scatter.5.cloned.1.call-done = f32[16,3072]{1,0:T(8,128)} async-done(((f32[128,3072]{1,0:T(8,128)}), f32[16,3072]{1,0:T(8,128)}) %reduce-scatter.5.cloned.1.call-update) | async-done | bytes 196624 | tf_op jit(solution)/shard_map/reduce_scatter | solution.py:35
  145.7 0.0 copy-done.1
  145.7 1.1 fusion.7
  146.8 0.0 slice-start
  146.8 0.8 stack.2
  147.5 0.0 slice-start.1
  147.5 140.1 %all_to_all.10 = f32[32,16,3072]{2,1,0:T(8,128)S(1)} all-to-all(f32[32,16,3072]{2,1,0:T(8,128)S(1)} %stack.2), channel_id=1, replica_groups=mesh['row_0'=4,'row_1'=8,'col_0'=4,'col_1'=2] {'row_0','row_1'}, dimensions={0} | all-to-all | bytes 12582912 | tf_op jit(solution)/shard_map/all_to_all | solution.py:66
  287.7 0.0 copy-start
  287.7 2.6 copy-done
  290.3 0.0 slice-done
  290.3 0.0 slice-done.1
  290.3 11.0 %fusion = f32[8,64,384]{2,1,0:T(8,128)} fusion(f32[8,64,3072]{2,1,0:T(8,128)S(1)} %bitcast.17, f32[384,3072]{1,0:T(8,128)S(1)} %bitcast.20), kind=kOutput, calls=%fused_computation | convolution fusion | flops 7247757312 | bytes 11796480 | tf_op jit(solution)/shard_map/dot_general | solution.py:75
  301.3 13.4 %all-to-all-start.1 = ((f32[8,64,384]{2,1,0:T(8,128)}), f32[8,64,384]{2,1,0:T(8,128)S(1)}, u32[]{:S(2)}, u32[]{:S(2)}) async-start(f32[8,64,384]{2,1,0:T(8,128)} %fusion), calls=%async_computation.3 | async-start | bytes 1572864 | tf_op jit(solution)/shard_map/all_to_all | solution.py:46
  314.7 13.6 %convolution_bitcast_fusion = f32[384,3072]{0,1:T(8,128)} fusion(f32[512,3072]{1,0:T(8,128)} %bitcast.18, f32[512,384]{1,0:T(8,128)S(1)} %bitcast.22), kind=kOutput, calls=%fused_computation.2 | convolution fusion | flops 7247757312 | bytes 11796480 | tf_op jit(solution)/shard_map/dot_general | solution.py:67
  328.3 6.0 %copy.10 = f32[384,3072]{1,0:T(8,128)} copy(f32[384,3072]{0,1:T(8,128)} %convolution_bitcast_fusion) | data formatting | bytes 9437184
  334.3 0.0 all-to-all-done.1
  334.3 0.7 reduce_sum.9
  (1 shorter events, 0.0 us)
Async XLA Ops:
  7.2 99.4 %reduce-scatter.3.cloned.1.call-start = ((), (), s32[]{:S(2)}) async-start(), calls=%async_computation.4 | async-start | bytes 7864320 | tf_op jit(solution)/shard_map/reduce_scatter | solution.py:35
  39.2 106.5 %copy-start.1 = (f32[16,3072]{1,0:T(8,128)S(1)}, f32[16,3072]{1,0:T(8,128)}, u32[]{:S(2)}) copy-start(f32[16,3072]{1,0:T(8,128)} %param.5) | copy-start | bytes 589828
  39.2 106.5 %reduce-scatter.5.cloned.1.call-start = ((), (), s32[]{:S(2)}) async-start(), calls=%async_computation.5 | async-start | bytes 1769472 | tf_op jit(solution)/shard_map/reduce_scatter | solution.py:35
  146.8 143.6 %slice-start = ((s8[4718592]{0:T(1024)(128)(4,1)}), s8[4194304]{0:T(1024)(128)(4,1)S(1)}, s32[]{:S(2)}) async-start(s8[4718592]{0:T(1024)(128)(4,1)} %bitcast.19), calls=%async_computation.6 | async-start | bytes 8388608
  147.5 142.8 %slice-start.1 = ((s8[4718592]{0:T(1024)(128)(4,1)}), s8[524288]{0:T(1024)(128)(4,1)S(1)}, s32[]{:S(2)}) async-start(s8[4718592]{0:T(1024)(128)(4,1)} %bitcast.19), calls=%async_computation.7 | async-start | bytes 1048576
  287.7 2.6 copy-start
  301.3 33.0 %all-to-all-start.1 = ((f32[8,64,384]{2,1,0:T(8,128)}), f32[8,64,384]{2,1,0:T(8,128)S(1)}, u32[]{:S(2)}, u32[]{:S(2)}) async-start(f32[8,64,384]{2,1,0:T(8,128)} %fusion), calls=%async_computation.3 | async-start | bytes 1572864 | tf_op jit(solution)/shard_map/all_to_all | solution.py:46
Sparse Core Ops, SparseCore 0:
  39.3 67.1 reduce-scatter.2
  109.1 36.5 reduce-scatter.4
